TPU v7x, 32 devices: a whole 2x2x4 slice. The times are simulated.
32 devices in a mesh: gx: 4 (over z), gy: 8 (over y, x, core).
Axes of the slice: x: 2, y: 2, z: 4, core: 2. Of those that a mesh axis runs over, the one named last changes fastest.
Arguments:
- rhs: float32 [4, 8, 1, 3, 200, 128], P('gx', 'gy'), may hold values from -25 to 25
- stiff_inverse: bfloat16 [4, 8, 1, 1200, 1200], P('gx', 'gy'), may hold values from -2 to 6, as said below
- schur: bfloat16 [4, 8, 1, 1200, 1200], P('gx', 'gy'), may hold values from -2 to 6, as said below
- phi: bfloat16 [4, 8, 1, 24, 1200], P('gx', 'gy'), may hold values from -0.1875 to 0.1875
- coarse_inverse: float32 [192, 192], P(('gx', 'gy')), may hold values from -2 to 6, as said below
- incidence: int32 [4, 8, 1, 8], P('gx', 'gy'), may hold values from 0 to 63, as said below
- pairing: int32 [4, 8, 1, 3, 200], P('gx', 'gy'), may hold values from 0 to 199, as said below
Outputs:
- multipliers: float32 [4, 8, 1, 3, 200, 128], P('gx', 'gy')
- reduction: float32 [128], replicated
Inputs may be any that keep to these rules, and one draw needn't show every extreme that they name: `stiff_inverse`: each block is symmetric positive definite. `schur`: each block is symmetric positive definite. `coarse_inverse`: symmetric positive definite. `incidence`: the corners of the subdomain grid, periodic in the first two dimensions, under an arbitrary numbering of the 64 nodes: corner c of subdomain (x, y, z) is the grid point (x + c % 2, y + (c // 2) % 2, z + c // 4), and subdomains that share a grid point name the same node. `pairing`: each row over the last dimension is a permutation of 0 to 199.
All inputs are finite; a program needn't handle non-finite values.
Results may differ from a plain program's by a relative error of at most 0.0027.
Values sent between devices are 32-bit elements; how exact they have to be, the bound alone decides.
A program may use at most 64 MiB of HBM per device.

v0:
```python
import functools

import jax
import jax.numpy as jnp
from jax import lax
from jax.experimental import pallas as pl
from jax.experimental.pallas import tpu as pltpu
from jax.sharding import PartitionSpec as P

ITERS = 2
EXCHANGES = 2 * ITERS
SUMS = 2 * ITERS + 1
GROUP = 8
MESH = pl.DeviceIdType.MESH
F32 = jnp.float32
BF16 = jnp.bfloat16


def split(value, parts):
    pieces = []
    for _ in range(parts):
        piece = value.astype(BF16)
        pieces.append(piece)
        value = value - piece.astype(F32)
    return pieces


def narrow_dot(matrix, value, parts):
    width = value.shape[1]
    product = jnp.dot(
        matrix, jnp.concatenate(split(value, parts), axis=1), preferred_element_type=F32
    )
    total = product[:, (parts - 1) * width :]
    for part in range(parts - 2, -1, -1):
        total = total + product[:, part * width : (part + 1) * width]
    return total


def full_dot(left, right):
    return jnp.dot(left, right, precision=lax.Precision.HIGHEST, preferred_element_type=F32)


def window(face, faces):
    start = face * faces // 128 * 128
    offset = face * faces - start
    return start, offset, -(-(offset + faces) // 128) * 128


def square_window(face, faces):
    start = face * faces // 128 * 128
    offset = face * faces - start
    return start, offset, -(-(offset + faces) // 256) * 256


def kernel(
    nx, ny, rhs_hbm, stiff_hbm, schur_hbm, phi_ref, cinv_ref, inc_ref, pair_ref,
    mult_ref, reduction_ref,
    rhs_v, stiff, schur, phi_f, phi_p, phi_t, near_t, near_phi, got_rhs, got_pair, got,
    field, way, image, sums_out, sums_in, ids_out, ids_in, cinv_in, cinv, chosen, assemble,
    load_x, load_y,
    local_sem, setup_send, setup_recv, face_send, face_recv, sum_send, sum_recv,
    all_send, all_recv, load_send, load_recv,
):
    n = nx * ny
    faces = rhs_v.shape[1]
    interface = stiff.shape[0]
    coarse = cinv.shape[0]
    ix, iy = lax.axis_index("gx"), lax.axis_index("gy")
    me = ix * ny + iy
    up_x, down_x = lax.rem(ix + 1, nx), lax.rem(ix + nx - 1, nx)
    up_y, down_y = lax.rem(iy + 1, ny), lax.rem(iy + ny - 1, ny)
    across = [(down_x, iy), (up_x, iy), (ix, down_y), (ix, up_y)]
    rows = [pl.ds(f * faces, faces) for f in range(6)]

    loads = [
        pltpu.make_async_copy(rhs_hbm, rhs_v, local_sem.at[0]),
        pltpu.make_async_copy(schur_hbm, schur, local_sem.at[1]),
        pltpu.make_async_copy(stiff_hbm, stiff, local_sem.at[2]),
    ]
    for copy in loads:
        copy.start()

    ways_x = [ix] + [lax.rem(ix + d, nx) for d in range(1, nx)]
    ways_y = [iy] + [lax.rem(iy + d, ny) for d in range(1, ny)]
    peers_x = [(x, iy) for x in ways_x[1:]]
    peers_y = [(ix, y) for y in ways_y[1:]]

    def each_peer(act):
        if n <= 64:
            for x in range(nx):
                for y in range(ny):
                    if x or y:
                        act((ways_x[x], ways_y[y]))
            return

        def step(k, carry):
            other = lax.rem(me + k, n)
            act((lax.div(other, ny), lax.rem(other, ny)))
            return carry

        lax.fori_loop(1, n, step, 0)

    barrier = pltpu.get_barrier_semaphore()
    each_peer(lambda target: pl.semaphore_signal(
        barrier, inc=1, device_id=target, device_id_type=MESH))

    corners = phi_f.shape[0]
    row = lax.broadcasted_iota(jnp.int32, (corners, corners), 0)
    col = lax.broadcasted_iota(jnp.int32, (corners, corners), 1)
    nodes = corners // 3
    side, half_rows = nodes // 2, corners // 2
    inner = lax.rem(row, half_rows)
    corner = lax.div(row, half_rows) + 2 * lax.rem(inner, side)
    order = jnp.where(col == 3 * corner + lax.div(inner, side), 1.0, 0.0)
    phi_f[...] = jnp.dot(order.astype(BF16), phi_ref[...], preferred_element_type=F32)
    ids = jnp.broadcast_to(inc_ref[...].astype(F32), (nodes, nodes))
    row = lax.broadcasted_iota(jnp.int32, (nodes, nodes), 0)
    col = lax.broadcasted_iota(jnp.int32, (nodes, nodes), 1)
    diag = col == lax.div(row, side) + 2 * lax.rem(row, side)
    ids = jnp.sum(jnp.where(diag, ids, 0.0), axis=1, keepdims=True)
    ids = jnp.broadcast_to(ids, ids_out.shape)
    ids_out[...] = ids
    ids_in[iy, ix] = ids
    cinv_in[iy, ix] = cinv_ref[...]

    loads[0].wait()
    pl.semaphore_wait(barrier, n - 1)

    def send(src, dst, send_sem, recv_sem, target):
        copy = pltpu.make_async_remote_copy(
            src_ref=src, dst_ref=dst, send_sem=send_sem, recv_sem=recv_sem,
            device_id=target, device_id_type=MESH,
        )
        copy.start()
        return copy

    def to_all(src, slots, send_sem, recv_sem):
        each_peer(lambda target: send(src, slots.at[me], send_sem, recv_sem, target))

    def to_line(src, dst, send_sem, recv_sem, targets):
        for target in targets:
            send(src, dst, send_sem, recv_sem, target)

    def wait_all(slots, sem):
        whole = slots.at[pl.ds(0, slots.shape[0] - 1)]
        pltpu.make_async_copy(whole, whole, sem).wait()

    setup = []
    for a in range(2):
        setup.append(send(pair_ref, got_pair.at[a], setup_send.at[a], setup_recv.at[a],
                          across[2 * a + 1]))
    for a in range(2):
        setup.append(send(rhs_v.at[a], got_rhs.at[a], setup_send.at[2 + a],
                          setup_recv.at[2 + a], across[2 * a + 1]))
    for f in range(4):
        start, _, width = window(f, faces)
        partner = f ^ 1
        setup.append(send(phi_f.at[:, pl.ds(start, width)],
                          near_phi.at[partner, :, pl.ds(0, width)],
                          setup_send.at[4 + f], setup_recv.at[4 + partner], across[f]))
    to_line(ids_out, ids_in.at[iy, ix], all_send.at[0], all_recv.at[0], peers_x)
    to_line(cinv_ref, cinv_in.at[iy, ix], all_send.at[1], all_recv.at[1], peers_x)

    def turned(pair_row, offset, width):
        lanes = lax.broadcasted_iota(jnp.int32, (1, width), 1)
        if width > faces:
            pair_row = jnp.concatenate(
                [pair_row, jnp.zeros((1, width - faces), jnp.int32)], axis=1
            )
        if offset:
            pair_row = pltpu.roll(pair_row, offset, axis=1)
        inside = (lanes >= offset) & (lanes < offset + faces)
        target = jnp.where(inside, pair_row + offset, lanes)
        place = lax.broadcasted_iota(jnp.int32, (width, width), 0)
        return jnp.where(place == target, 1.0, 0.0)

    turns = []
    for a in range(2):
        setup[a].wait_recv()
        start, offset, width = square_window(2 * a, faces)
        by_col = turned(got_pair[a, a : a + 1, :], offset, width)
        turns.append((start, width, by_col.T.astype(BF16), by_col.astype(BF16)))

    def reorder(matrix):
        for start, width, by_row, _ in turns:
            band = matrix[pl.ds(start, width), :]
            matrix[pl.ds(start, width), :] = jnp.dot(
                by_row, band, preferred_element_type=F32
            ).astype(BF16)
        for start, width, _, by_col in turns:
            band = matrix[:, pl.ds(start, width)]
            matrix[:, pl.ds(start, width)] = jnp.dot(
                band, by_col, preferred_element_type=F32
            ).astype(BF16)

    wait_all(ids_in.at[iy], all_recv.at[0])
    wait_all(cinv_in.at[iy], all_recv.at[1])
    to_line(ids_in.at[iy], ids_in.at[iy], all_send.at[2], all_recv.at[2], peers_y)
    to_line(cinv_in.at[iy], cinv_in.at[iy], all_send.at[3], all_recv.at[3], peers_y)
    loads[1].wait()
    reorder(schur)

    def apply_local(matrix, low, k):
        sent = []
        for half in range(3):
            part = pl.ds(2 * half * faces, 2 * faces)
            image[k, part, :] = jnp.dot(matrix[part, :], low, preferred_element_type=F32)
            if half < 2:
                for f in (2 * half, 2 * half + 1):
                    sent.append(send(image.at[k, rows[f]], got.at[k, f ^ 1],
                                     face_send.at[k, f], face_recv.at[k, f ^ 1], across[f]))
        return sent

    def start_sum(partial, k):
        total = jnp.sum(partial, axis=0, keepdims=True)
        sums_out[k] = total
        sums_in[k, me] = total
        to_all(sums_out.at[k], sums_in.at[k], sum_send.at[k], sum_recv.at[k])

    def finish_sum(k):
        wait_all(sums_in.at[k], sum_recv.at[k])
        return jnp.sum(sums_in[k], axis=0)

    def wait_faces(k):
        for f in range(4):
            pltpu.make_async_copy(got.at[k, f], got.at[k, f], face_recv.at[k, f]).wait()

    zeros = jnp.zeros((2 * faces, field.shape[1]), F32)
    for a in range(2):
        setup[2 + a].wait_recv()
        field[rows[2 * a], :] = -got_rhs[a]
        field[rows[2 * a + 1], :] = rhs_v[a]
    field[pl.ds(4 * faces, 2 * faces), :] = zeros
    for k in range(ITERS):
        way[k, pl.ds(4 * faces, 2 * faces), :] = zeros

    sent = []

    def precondition(k, s):
        half = 0.5 * field[...]
        sent.extend(apply_local(schur, half.astype(BF16), k))
        start_sum(half * image[k], s)

    precondition(0, 0)

    loads[2].wait()
    reorder(stiff)
    phi_p[...] = phi_f[...].astype(BF16)
    for start, width, _, by_col in turns:
        phi_p[:, pl.ds(start, width)] = jnp.dot(
            phi_p[:, pl.ds(start, width)], by_col, preferred_element_type=F32
        ).astype(BF16)
    phi_t[...] = phi_p[...].astype(F32).T.astype(BF16)

    group = min(GROUP, ny)
    width = nx * half_rows

    def dof_rows(block):
        return jnp.concatenate(
            [3.0 * block[h * side : (h + 1) * side] + i for h in range(2) for i in range(3)],
            axis=0,
        )

    def placed(g):
        block = ids_in[pl.ds(g * group, group)].reshape(group * nx // 2, 2, nodes, 128)
        block = jnp.concatenate(
            [3.0 * block[:, b, 0:side] + i for b in range(2) for i in range(3)], axis=1
        )
        line = block.reshape(group * width, 128).T[0:1]
        spot = lax.broadcasted_iota(jnp.int32, (coarse, group * width), 0).astype(F32)
        return jnp.where(spot == line, 1.0, 0.0).astype(BF16)

    def prepare_coarse():
        for f in range(4):
            _, offset, width = window(f ^ 1, faces)
            setup[4 + (f ^ 1)].wait_recv()
            tall = near_phi[f, :, pl.ds(0, width)].T[offset : offset + faces]
            if f % 2:
                by_row = turned(pair_ref[f // 2 : f // 2 + 1, :], 0, faces).T
                tall = jnp.dot(by_row.astype(BF16), tall.astype(BF16),
                               preferred_element_type=F32)
            near_t[f] = tall.astype(BF16)
        wait_all(ids_in, all_recv.at[2])
        if ny == group:
            assemble[...] = placed(0)
        wait_all(cinv_in, all_recv.at[3])
        block_rows = 4 * cinv_in.shape[2]
        for x in range(nx):
            def pack(g, carry):
                block = jnp.concatenate([cinv_in[4 * g + i, x] for i in range(4)], axis=0)
                place = (x * (ny // 4) + g) * block_rows
                cinv[pl.ds(pl.multiple_of(place, 8), block_rows), :] = block
                return carry

            lax.fori_loop(0, ny // 4, pack, 0, unroll=ny <= 8)
        picks = []
        for gx, gy in across + [(ix, iy)]:
            dofs = dof_rows(ids_in[gy, gx])[:, 0:1]
            spot = lax.broadcasted_iota(jnp.int32, (corners, coarse), 1).astype(F32)
            picks.append(jnp.where(spot == dofs, 1.0, 0.0))
        pick = jnp.concatenate(picks, axis=0).astype(BF16)
        chosen[...] = narrow_dot(pick, cinv[...], 3)

    energy = start_energy = previous = None
    alphas = []
    for it in range(ITERS):
        k = 2 * it
        wait_faces(k)
        if it:
            following = finish_sum(2 * it)
            ratio = following / energy
            energy = following
        for f in range(4):
            moved = 0.5 * (image[k, rows[f], :] - got[k, f])
            if it:
                moved = moved + ratio * way[it - 1, rows[f], :]
            way[it, rows[f], :] = moved
        walk = way[it]
        corner_load = narrow_dot(phi_p[...], walk, 2)
        load_x[it, ix] = corner_load
        to_line(load_x.at[it, ix], load_x.at[it, ix], load_send.at[it], load_recv.at[it],
                peers_x)
        sent.extend(apply_local(stiff, walk.astype(BF16), k + 1))
        start_sum(walk * image[k + 1], 2 * it + 1)
        wait_all(load_x.at[it], load_recv.at[it])
        for pair in range(nx // 2):
            joined = [
                load_x[it, x, 0:half_rows] + load_x[it, (x - 1) % nx, half_rows:corners]
                for x in (2 * pair, 2 * pair + 1)
            ]
            load_y[it, iy, pl.ds(pair * corners, corners)] = jnp.concatenate(joined, axis=0)
        to_line(load_y.at[it, iy], load_y.at[it, iy], load_send.at[ITERS + it],
                load_recv.at[ITERS + it], peers_y)
        if it == 0:
            prepare_coarse()
            energy = start_energy = finish_sum(0)
        wait_all(load_y.at[it], load_recv.at[ITERS + it])

        def gather(g, total):
            if ny > group:
                assemble[...] = placed(g)
            block = load_y[it, pl.ds(g * group, group)].reshape(group * width, -1)
            return total + narrow_dot(assemble[...], block, 3)

        coarse_load = lax.fori_loop(
            0, ny // group, gather, jnp.zeros((coarse, field.shape[1]), F32)
        )
        solution_rows = full_dot(cinv[...], coarse_load)
        near = full_dot(chosen[...], coarse_load)
        coarse_part = jnp.sum(coarse_load * solution_rows, axis=0, keepdims=True)
        own = narrow_dot(phi_t[...], near[4 * corners :], 2)
        wait_faces(k + 1)
        alpha = energy / (finish_sum(2 * it + 1) + coarse_part)
        alphas.append(alpha)
        for f in range(4):
            other = narrow_dot(near_t[f], near[f * corners : (f + 1) * corners], 2)
            jump = (image[k + 1, rows[f], :] - got[k + 1, f]) + (
                own[f * faces : (f + 1) * faces] - other
            )
            field[rows[f], :] = field[rows[f], :] - alpha * jump
        if it + 1 < ITERS:
            precondition(k + 2, 2 * it + 2)
        else:
            half = 0.5 * field[...]
            product = jnp.dot(schur[...], half.astype(BF16), preferred_element_type=F32)
            start_sum(half * product, 2 * it + 2)

    for a in range(2):
        total = alphas[0] * way[0, rows[2 * a + 1], :]
        for it in range(1, ITERS):
            total = total + alphas[it] * way[it, rows[2 * a + 1], :]
        mult_ref[a] = total
    mult_ref[2] = jnp.zeros(mult_ref.shape[1:], F32)

    for copy in setup + sent:
        copy.wait_send()
    wait_all(ids_in.at[iy], all_send.at[0])
    wait_all(cinv_in.at[iy], all_send.at[1])
    wait_all(ids_in, all_send.at[2])
    wait_all(cinv_in, all_send.at[3])
    for it in range(ITERS):
        wait_all(load_x.at[it], load_send.at[it])
        wait_all(load_y.at[it], load_send.at[ITERS + it])
    reduction_ref[...] = finish_sum(SUMS - 1) / start_energy
    for k in range(SUMS):
        wait_all(sums_in.at[k], sum_send.at[k])


def local(nx, ny, rhs, stiff_inverse, schur, phi, coarse_inverse, incidence, pairing):
    n = nx * ny
    faces, cases = rhs.shape[4], rhs.shape[5]
    interface = stiff_inverse.shape[3]
    corners = phi.shape[3]
    coarse_rows, coarse = coarse_inverse.shape
    nodes = incidence.shape[3]
    group = min(GROUP, ny)
    wide = max(window(f, faces)[2] for f in range(4))
    vmem = pl.BlockSpec(memory_space=pltpu.VMEM)
    anywhere = pl.BlockSpec(memory_space=pl.ANY)
    dma = pltpu.SemaphoreType.DMA
    multipliers, reduction = pl.pallas_call(
        functools.partial(kernel, nx, ny),
        out_shape=(
            jax.ShapeDtypeStruct((3, faces, cases), F32),
            jax.ShapeDtypeStruct((1, cases), F32),
        ),
        in_specs=[anywhere] * 3 + [vmem] * 4,
        out_specs=(vmem, vmem),
        scratch_shapes=[
            pltpu.VMEM((3, faces, cases), F32),
            pltpu.VMEM((interface, interface), BF16),
            pltpu.VMEM((interface, interface), BF16),
            pltpu.VMEM((corners, interface), F32),
            pltpu.VMEM((corners, interface), BF16),
            pltpu.VMEM((interface, corners), BF16),
            pltpu.VMEM((4, faces, corners), BF16),
            pltpu.VMEM((4, corners, wide), F32),
            pltpu.VMEM((2, faces, cases), F32),
            pltpu.VMEM((2, 3, faces), jnp.int32),
            pltpu.VMEM((EXCHANGES, 4, faces, cases), F32),
            pltpu.VMEM((interface, cases), F32),
            pltpu.VMEM((ITERS, interface, cases), F32),
            pltpu.VMEM((EXCHANGES, interface, cases), F32),
            pltpu.VMEM((SUMS, 1, cases), F32),
            pltpu.VMEM((SUMS, n, 1, cases), F32),
            pltpu.VMEM((nodes, 128), F32),
            pltpu.VMEM((ny, nx, nodes, 128), F32),
            pltpu.VMEM((ny, nx, coarse_rows, coarse), F32),
            pltpu.VMEM((coarse, coarse), F32),
            pltpu.VMEM((5 * corners, coarse), F32),
            pltpu.VMEM((coarse, group * nx * corners // 2), BF16),
            pltpu.VMEM((ITERS, nx, corners, cases), F32),
            pltpu.VMEM((ITERS, ny, nx * corners // 2, cases), F32),
            dma((3,)),
            dma((8,)),
            dma((8,)),
            dma((EXCHANGES, 4)),
            dma((EXCHANGES, 4)),
            dma((SUMS,)),
            dma((SUMS,)),
            dma((4,)),
            dma((4,)),
            dma((2 * ITERS,)),
            dma((2 * ITERS,)),
        ],
        compiler_params=pltpu.CompilerParams(
            collective_id=0, has_side_effects=True, vmem_limit_bytes=67043328
        ),
    )(
        rhs.reshape(3, faces, cases),
        stiff_inverse.reshape(interface, interface),
        schur.reshape(interface, interface),
        phi.reshape(corners, interface),
        coarse_inverse,
        incidence.reshape(1, nodes),
        pairing.reshape(3, faces),
    )
    return multipliers.reshape(rhs.shape), reduction.reshape(cases)


def solution(mesh):
    nx, ny = mesh.shape["gx"], mesh.shape["gy"]
    return jax.shard_map(
        functools.partial(local, nx, ny),
        mesh=mesh,
        in_specs=(
            P("gx", "gy", None, None, None, None),
            P("gx", "gy", None, None, None),
            P("gx", "gy", None, None, None),
            P("gx", "gy", None, None, None),
            P(("gx", "gy"), None),
            P("gx", "gy", None, None),
            P("gx", "gy", None, None, None),
        ),
        out_specs=(P("gx", "gy", None, None, None, None), P()),
        check_vma=False,
    )
```

profile of v0, /device:TPU:0, one launch (start us, length us, event | category | flops | bytes accessed | tf_op | source)
XLA Modules:
  0.0 65.0 jit_solution(13163209788840468170)
XLA Ops:
  0.6 1.3 %copy.11 = s32[1,1,1,3,200]{4,3,2,1,0:T(4,128)} copy(s32[1,1,1,3,200]{4,2,3,1,0:T(1,128)} %param.13) | data formatting | bytes 4800
  1.9 60.2 %shard_map.86 = (f32[3,200,128]{2,1,0:T(8,128)}, f32[1,128]{1,0:T(1,128)}) custom-call(f32[3,200,128]{2,1,0:T(8,128)} %bitcast.13, bf16[1200,1200]{1,0:T(8,128)(2,1)} %bitcast.10, bf16[1200,1200]{1,0:T(8,128)(2,1)} %bitcast.11, bf16[24,1200]{1,0:T(8,128)(2,1)} %bitcast.14, f32[6,192]{1,0:T(8,128)} %cinv_ref.1, s32[1,8]{1,0:T(1,128)} %bitcast.16, ...), custom_call_target="tpu_custom_call" | custom-call | tf_op jit(solution)/shard_map/pallas_call | solution.py:401
  62.1 1.7 %copy.14 = f32[1,1,1,3,200,128]{5,4,3,2,1,0:T(8,128)} copy(f32[1,1,1,3,200,128]{5,4,3,2,1,0:T(8,128)} %bitcast.12) | data formatting | bytes 614400
  63.8 1.2 %copy.15 = f32[128]{0:T(128)} copy(f32[128]{0:T(128)} %bitcast.17) | data formatting | bytes 1024
where the time goes:
time: 65.2 us; the launch traced here: 65 us
  Pallas kernels  60.2 us (92%)
  local copies, waits for them, and re-layouts  4.17 us (6%)
    pallas_call x1, Pallas kernels, local(): pl.pallas_call(functools.partial(kernel, nx, ny), out_shape=(jax.ShapeDty...  60.2 us
    unnamed x3, local copies, waits for them, and re-layouts  4.17 us

commit v1 on v0

v1 whole, which is shorter than its diff:
```python
import functools

import jax
import jax.numpy as jnp
from jax import lax
from jax.experimental import pallas as pl
from jax.experimental.pallas import tpu as pltpu
from jax.sharding import PartitionSpec as P

ITERS = 2
EXCHANGES = 2 * ITERS
SUMS = 2 * ITERS + 1
MESH = pl.DeviceIdType.MESH
F32 = jnp.float32
BF16 = jnp.bfloat16


def split(value, parts):
    pieces = []
    for _ in range(parts):
        piece = value.astype(BF16)
        pieces.append(piece)
        value = value - piece.astype(F32)
    return pieces


def narrow_dot(matrix, value, parts):
    width = value.shape[1]
    product = jnp.dot(
        matrix, jnp.concatenate(split(value, parts), axis=1), preferred_element_type=F32
    )
    total = product[:, (parts - 1) * width :]
    for part in range(parts - 2, -1, -1):
        total = total + product[:, part * width : (part + 1) * width]
    return total


def window(face, faces):
    start = face * faces // 128 * 128
    offset = face * faces - start
    return start, offset, -(-(offset + faces) // 128) * 128


def square_window(face, faces):
    start = face * faces // 128 * 128
    offset = face * faces - start
    return start, offset, -(-(offset + faces) // 256) * 256


def kernel(
    nx, ny, rhs_hbm, stiff_hbm, schur_hbm, phi_ref, cinv_ref, inc_ref, pair_ref,
    mult_hbm, reduction_ref,
    rhs_v, stiff, schur, phi_f, spread, spread_t, near_phi, got_rhs, got_pair, got,
    field, way, image, sums_out, sums_in, ids_out, ids_in, cinv_out, cinv_in, middle, inverse,
    part_out, part_in, part_own, load_x, load_y, loads_v, solved, lift, mult_v,
    local_sem, setup_send, setup_recv, face_send, face_recv, sum_send, sum_recv,
    all_send, all_recv, part_send, part_recv, load_send, load_recv,
):
    n = nx * ny
    faces = rhs_v.shape[1]
    cases = rhs_v.shape[2]
    jumps = 4 * faces
    coarse = cinv_in.shape[3]
    slots = n * 8
    ix, iy = lax.axis_index("gx"), lax.axis_index("gy")
    me = ix * ny + iy

    def at(dx, dy):
        return lax.rem(ix + (dx + nx), nx), lax.rem(iy + (dy + ny), ny)

    across = [at(-1, 0), at(1, 0), at(0, -1), at(0, 1)]
    rows = [pl.ds(f * faces, faces) for f in range(6)]

    loads = [
        pltpu.make_async_copy(rhs_hbm, rhs_v, local_sem.at[0]),
        pltpu.make_async_copy(schur_hbm, schur, local_sem.at[1]),
        pltpu.make_async_copy(stiff_hbm, stiff, local_sem.at[2]),
    ]
    for copy in loads:
        copy.start()

    ways_x = [at(d, 0)[0] for d in range(nx)]
    ways_y = [at(0, d)[1] for d in range(ny)]
    peers_x = [(x, iy) for x in ways_x[1:]]
    peers_y = [(ix, y) for y in ways_y[1:]]

    def each_peer(act):
        if n <= 64:
            for x in range(nx):
                for y in range(ny):
                    if x or y:
                        act((ways_x[x], ways_y[y]))
            return

        def step(k, carry):
            other = lax.rem(me + k, n)
            act((lax.div(other, ny), lax.rem(other, ny)))
            return carry

        lax.fori_loop(1, n, step, 0)

    barrier = pltpu.get_barrier_semaphore()
    each_peer(lambda target: pl.semaphore_signal(
        barrier, inc=1, device_id=target, device_id_type=MESH))

    corners = phi_ref.shape[0]
    row = lax.broadcasted_iota(jnp.int32, (32, corners), 0)
    col = lax.broadcasted_iota(jnp.int32, (32, corners), 1)
    point, inner = lax.div(row, 8), lax.rem(row, 8)
    source = 3 * (point + 4 * lax.div(inner, 3)) + lax.rem(inner, 3)
    order = jnp.where((col == source) & (inner < 6), 1.0, 0.0)
    phi_f[...] = jnp.dot(order.astype(BF16), phi_ref[...], preferred_element_type=F32)
    row = lax.broadcasted_iota(jnp.int32, (8, 8), 0)
    col = lax.broadcasted_iota(jnp.int32, (8, 8), 1)
    ids = jnp.broadcast_to(inc_ref[...].astype(F32), (8, 8))
    ids = jnp.sum(jnp.where(col == 4 * lax.div(row, 3), ids, 0.0), axis=1, keepdims=True)
    row = lax.broadcasted_iota(jnp.int32, ids_out.shape, 0)
    ids = 3.0 * jnp.broadcast_to(ids, ids_out.shape) + lax.rem(row, 3).astype(F32)
    ids = jnp.where(row < 6, ids, -1.0)
    ids_out[...] = ids
    ids_in[iy, ix] = ids
    own = jnp.concatenate([cinv_ref[...], jnp.zeros((2, coarse), F32)], axis=0)
    cinv_out[...] = own
    cinv_in[iy, ix] = own

    loads[0].wait()
    pl.semaphore_wait(barrier, n - 1)

    def send(src, dst, send_sem, recv_sem, target):
        copy = pltpu.make_async_remote_copy(
            src_ref=src, dst_ref=dst, send_sem=send_sem, recv_sem=recv_sem,
            device_id=target, device_id_type=MESH,
        )
        copy.start()
        return copy

    def to_all(src, slots, send_sem, recv_sem):
        each_peer(lambda target: send(src, slots.at[me], send_sem, recv_sem, target))

    def to_line(src, dst, send_sem, recv_sem, targets):
        for target in targets:
            send(src, dst, send_sem, recv_sem, target)

    def wait_all(slots, sem):
        whole = slots.at[pl.ds(0, slots.shape[0] - 1)]
        pltpu.make_async_copy(whole, whole, sem).wait()

    setup = []
    for a in range(2):
        setup.append(send(pair_ref.at[a], got_pair.at[a], setup_send.at[a], setup_recv.at[a],
                          across[2 * a + 1]))
    for a in range(2):
        setup.append(send(rhs_v.at[a], got_rhs.at[a], setup_send.at[2 + a],
                          setup_recv.at[2 + a], across[2 * a + 1]))
    for f in range(4):
        start, _, width = window(f, faces)
        partner = f ^ 1
        setup.append(send(phi_f.at[:, pl.ds(start, width)],
                          near_phi.at[partner, :, pl.ds(0, width)],
                          setup_send.at[4 + f], setup_recv.at[4 + partner], across[f]))
    to_line(ids_out, ids_in.at[iy, ix], all_send.at[0], all_recv.at[0], peers_x)
    to_line(cinv_out, cinv_in.at[iy, ix], all_send.at[1], all_recv.at[1], peers_x)

    def turned(pair_row, offset, width):
        lanes = lax.broadcasted_iota(jnp.int32, (1, width), 1)
        if width > faces:
            pair_row = jnp.concatenate(
                [pair_row, jnp.zeros((1, width - faces), jnp.int32)], axis=1
            )
        if offset:
            pair_row = pltpu.roll(pair_row, offset, axis=1)
        inside = (lanes >= offset) & (lanes < offset + faces)
        target = jnp.where(inside, pair_row + offset, lanes)
        place = lax.broadcasted_iota(jnp.int32, (width, width), 0)
        return jnp.where(place == target, 1.0, 0.0)

    turns = []
    for a in range(2):
        setup[a].wait_recv()
        start, offset, width = square_window(2 * a, faces)
        by_col = turned(got_pair[a], offset, width)
        turns.append((start, width, by_col.T.astype(BF16), by_col.astype(BF16)))

    def reorder(matrix):
        for start, width, by_row, _ in turns:
            band = matrix[pl.ds(start, width), :]
            matrix[pl.ds(start, width), :] = jnp.dot(
                by_row, band, preferred_element_type=F32
            ).astype(BF16)
        for start, width, _, by_col in turns:
            band = matrix[:, pl.ds(start, width)]
            matrix[:, pl.ds(start, width)] = jnp.dot(
                band, by_col, preferred_element_type=F32
            ).astype(BF16)

    loads[1].wait()
    reorder(schur)

    spread[pl.ds(0, 32), :] = phi_f[:, pl.ds(0, spread.shape[1])].astype(BF16)
    for start, width, _, by_col in turns:
        spread[pl.ds(0, 32), pl.ds(start, width)] = jnp.dot(
            spread[pl.ds(0, 32), pl.ds(start, width)], by_col, preferred_element_type=F32
        ).astype(BF16)
    spread[pl.ds(32, 128), :] = jnp.zeros((128, spread.shape[1]), BF16)

    def apply_local(matrix, low, k):
        sent = []
        for half in range(3):
            part = pl.ds(2 * half * faces, 2 * faces)
            image[k, part, :] = jnp.dot(matrix[part, :], low, preferred_element_type=F32)
            if half < 2:
                for f in (2 * half, 2 * half + 1):
                    sent.append(send(image.at[k, rows[f]], got.at[k, f ^ 1],
                                     face_send.at[k, f], face_recv.at[k, f ^ 1], across[f]))
        return sent

    def start_sum(partial, k):
        total = jnp.sum(partial, axis=0, keepdims=True)
        sums_out[k] = total
        sums_in[k, me] = total
        to_all(sums_out.at[k], sums_in.at[k], sum_send.at[k], sum_recv.at[k])

    def finish_sum(k):
        wait_all(sums_in.at[k], sum_recv.at[k])
        return jnp.sum(sums_in[k], axis=0)

    def wait_faces(k):
        for f in range(4):
            pltpu.make_async_copy(got.at[k, f], got.at[k, f], face_recv.at[k, f]).wait()

    zeros = jnp.zeros((2 * faces, cases), F32)
    for a in range(2):
        setup[2 + a].wait_recv()
        field[rows[2 * a], :] = -got_rhs[a]
        field[rows[2 * a + 1], :] = rhs_v[a]
    field[pl.ds(jumps, 2 * faces), :] = zeros
    for k in range(ITERS):
        way[k, pl.ds(jumps, 2 * faces), :] = zeros

    sent = []

    def precondition(k, s):
        half = 0.5 * field[...]
        sent.extend(apply_local(schur, half.astype(BF16), k))
        start_sum(half * image[k], s)

    def couple():
        for f in range(4):
            setup[4 + (f ^ 1)].wait_recv()
            start, offset, width = window(f, faces)
            _, other_offset, other_width = window(f ^ 1, faces)
            other = near_phi[f, :, pl.ds(0, other_width)]
            if f % 2:
                by_col = turned(pair_ref[f // 2], other_offset, other_width)
                other = jnp.dot(other.astype(BF16), by_col.astype(BF16),
                                preferred_element_type=F32)
            if other_width < width:
                other = jnp.concatenate(
                    [other, jnp.zeros((32, width - other_width), F32)], axis=1
                )
            both = other.shape[1]
            other = pltpu.roll(other, (offset - other_offset) % both, axis=1)
            lanes = lax.broadcasted_iota(jnp.int32, (32, both), 1)
            inside = (lanes >= offset) & (lanes < offset + faces)
            other = jnp.where(inside, -other, 0.0)[:, 0:width]
            spread[pl.ds(32 + 32 * f, 32), pl.ds(start, width)] = other.astype(BF16)

    def start_loads(k, it):
        value = narrow_dot(spread[:, pl.ds(0, jumps)], image[k, pl.ds(0, jumps), :], 2)

        def own(b, a):
            return 0.5 * value[8 * (2 * b + a) : 8 * (2 * b + a) + 8]

        def near(f, b, a):
            return 0.5 * value[32 + 32 * f + 8 * (2 * b + a) : 40 + 32 * f + 8 * (2 * b + a)]

        for b in range(2):
            line = jnp.concatenate([
                near(0, b, 0),
                own(b, 0) + near(0, b, 1) + near(2 + b, 1 - b, 0),
                own(b, 1) + near(1, b, 0) + near(2 + b, 1 - b, 1),
                near(1, b, 1),
            ], axis=0)
            if b:
                part_out[it, pl.ds(0, 32), :] = line
            else:
                part_own[it] = line
        part_out[it, pl.ds(32, 16), :] = jnp.concatenate([near(2, 0, 0), near(2, 0, 1)], axis=0)
        part_out[it, pl.ds(48, 16), :] = jnp.concatenate([near(3, 1, 0), near(3, 1, 1)], axis=0)
        for j, (start, size, dy) in enumerate(((0, 32, 1), (32, 16, -1), (48, 16, 2))):
            part = pl.ds(start, size)
            sent.append(send(part_out.at[it, part], part_in.at[it, part], part_send.at[it, j],
                             part_recv.at[it, j], at(0, dy)))

    def pass_loads(it):
        for j, (start, size) in enumerate(((0, 32), (32, 16), (48, 16))):
            part = part_in.at[it, pl.ds(start, size)]
            pltpu.make_async_copy(part, part, part_recv.at[it, j]).wait()
        line = part_own[it] + part_in[it, pl.ds(0, 32), :]
        inner = part_in[it, pl.ds(32, 16), :] + part_in[it, pl.ds(48, 16), :]
        edge = jnp.zeros((8, cases), F32)
        load_x[it, ix] = line + jnp.concatenate([edge, inner, edge], axis=0)
        to_line(load_x.at[it, ix], load_x.at[it, ix], load_send.at[it], load_recv.at[it],
                peers_x)

    def share_loads(it):
        wait_all(load_x.at[it], load_recv.at[it])
        for x in range(nx):
            total = load_x[it, (x + 1) % nx, pl.ds(0, 8), :]
            for a in range(3):
                total = total + load_x[it, (x - a) % nx, pl.ds(8 * a + 8, 8), :]
            load_y[it, iy, pl.ds(8 * x, 8), :] = total
        to_line(load_y.at[it, iy], load_y.at[it, iy], load_send.at[ITERS + it],
                load_recv.at[ITERS + it], peers_y)

    block = min(256, slots)
    blocks = slots // block

    def each_block(act):
        if blocks == 1:
            act(0)
            return

        def step(g, carry):
            act(pl.multiple_of(g * block, block))
            return carry

        lax.fori_loop(0, blocks, step, 0)

    def prepare_coarse():
        wait_all(ids_in, all_recv.at[2])
        wait_all(cinv_in, all_recv.at[3])
        per_y = nx * 8
        group = block // per_y

        def order_columns(part, start):
            first = start if isinstance(start, int) else lax.div(start, per_y)
            raw = cinv_in[pl.ds(first, group)].reshape(block, coarse)
            dofs = ids_in[...].reshape(slots, 128)[:, 0:1]
            spot = lax.broadcasted_iota(jnp.int32, (slots, coarse), 1).astype(F32)
            pick = jnp.where(spot == dofs, 1.0, 0.0).astype(BF16)
            middle[pl.ds(start, block), :] = lax.dot_general(
                split(raw, 2)[part], pick, (((1,), (1,)), ((), ())), preferred_element_type=F32
            ).astype(BF16)

        def order_rows(part, start):
            first = start if isinstance(start, int) else lax.div(start, per_y)
            dofs = ids_in[pl.ds(first, group)].reshape(block, 128)[:, 0:1]
            spot = lax.broadcasted_iota(jnp.int32, (block, slots), 1)
            device = lax.div(spot, 8)
            inner = lax.rem(spot, 8)
            device = lax.rem(device, nx) * ny + lax.div(device, nx)
            held = jnp.where(inner < 6, 6 * device + inner, -2).astype(F32)
            pick = jnp.where(held == dofs, 1.0, 0.0).astype(BF16)
            inverse[part, pl.ds(start, block), :] = jnp.dot(
                pick, middle[...], preferred_element_type=F32
            ).astype(BF16)

        for part in range(2):
            each_block(functools.partial(order_columns, part))
            each_block(functools.partial(order_rows, part))
        spread_t[...] = spread[:, pl.ds(0, jumps)].astype(F32).T.astype(BF16)

    def solve(it, ratio):
        wait_all(load_y.at[it], load_recv.at[ITERS + it])
        load = load_y[it].reshape(slots, cases)
        if it:
            load = load + ratio * loads_v[it - 1]
        loads_v[it] = load
        both = jnp.concatenate(split(load, 2), axis=1)

        def act(start):
            total = jnp.zeros((block, cases), F32)
            for part in (1, 0):
                product = jnp.dot(inverse[part, pl.ds(start, block), :], both,
                                  preferred_element_type=F32)
                total = total + product[:, cases:]
                total = total + product[:, 0:cases]
            first = start if isinstance(start, int) else lax.div(start, nx * 8)
            solved[pl.ds(first, block // (nx * 8))] = total.reshape(
                block // (nx * 8), nx, 8, cases)

        each_block(act)
        points = {}

        def point(dx, dy):
            if (dx, dy) not in points:
                x, y = at(dx, dy)
                points[dx, dy] = solved[y, x]
            return points[dx, dy]

        pieces = []
        for dx, dy in ((0, 0), (-1, 0), (1, 0), (0, -1), (0, 1)):
            pieces += [point(dx + a, dy + b) for b in range(2) for a in range(2)]
        lift[...] = narrow_dot(spread_t[...], jnp.concatenate(pieces, axis=0), 2)
        return jnp.sum(load * solved[...].reshape(slots, cases), axis=0, keepdims=True)

    precondition(0, 0)
    couple()
    energy = start_energy = None
    ratio = None
    alphas = []
    for it in range(ITERS):
        k = 2 * it
        start_loads(k, it)
        if it == 0:
            wait_all(ids_in.at[iy], all_recv.at[0])
            wait_all(cinv_in.at[iy], all_recv.at[1])
            to_line(ids_in.at[iy], ids_in.at[iy], all_send.at[2], all_recv.at[2], peers_y)
            to_line(cinv_in.at[iy], cinv_in.at[iy], all_send.at[3], all_recv.at[3], peers_y)
            loads[2].wait()
            reorder(stiff)
        pass_loads(it)
        if it:
            following = finish_sum(2 * it)
            ratio = following / energy
            energy = following
        wait_faces(k)
        for f in range(4):
            moved = 0.5 * (image[k, rows[f], :] - got[k, f])
            if it:
                moved = moved + ratio * way[it - 1, rows[f], :]
            way[it, rows[f], :] = moved
        walk = way[it]
        sent.extend(apply_local(stiff, walk.astype(BF16), k + 1))
        start_sum(walk * image[k + 1], 2 * it + 1)
        share_loads(it)
        if it == 0:
            prepare_coarse()
            energy = start_energy = finish_sum(0)
        coarse_part = solve(it, ratio)
        alpha = energy / (finish_sum(2 * it + 1) + coarse_part)
        alphas.append(alpha)
        wait_faces(k + 1)
        for f in range(4):
            jump = (image[k + 1, rows[f], :] - got[k + 1, f]) + lift[rows[f], :]
            field[rows[f], :] = field[rows[f], :] - alpha * jump
        if it + 1 < ITERS:
            precondition(k + 2, 2 * it + 2)
        else:
            half = 0.5 * field[...]
            product = jnp.dot(schur[...], half.astype(BF16), preferred_element_type=F32)
            start_sum(half * product, 2 * it + 2)

    for a in range(2):
        total = alphas[0] * way[0, rows[2 * a + 1], :]
        for it in range(1, ITERS):
            total = total + alphas[it] * way[it, rows[2 * a + 1], :]
        mult_v[a] = total
    mult_v[2] = jnp.zeros(mult_v.shape[1:], F32)
    result = pltpu.make_async_copy(mult_v, mult_hbm, local_sem.at[3])
    result.start()

    for copy in setup + sent:
        copy.wait_send()
    wait_all(ids_in.at[iy], all_send.at[0])
    wait_all(cinv_in.at[iy], all_send.at[1])
    wait_all(ids_in, all_send.at[2])
    wait_all(cinv_in, all_send.at[3])
    for it in range(ITERS):
        wait_all(load_x.at[it], load_send.at[it])
        wait_all(load_y.at[it], load_send.at[ITERS + it])
    for k in range(SUMS - 1):
        wait_all(sums_in.at[k], sum_send.at[k])
    result.wait()
    reduction_ref[...] = finish_sum(SUMS - 1) / start_energy
    wait_all(sums_in.at[SUMS - 1], sum_send.at[SUMS - 1])


def finish(mult_ref, reduction_ref, mult_out, reduction_out):
    mult_out[...] = mult_ref[...]
    reduction_out[...] = reduction_ref[...]


def local(nx, ny, rhs, stiff_inverse, schur, phi, coarse_inverse, incidence, pairing):
    n = nx * ny
    faces, cases = rhs.shape[4], rhs.shape[5]
    interface = stiff_inverse.shape[3]
    corners = phi.shape[3]
    coarse = coarse_inverse.shape[1]
    nodes = incidence.shape[3]
    slots = 8 * n
    wide = max(window(f, faces)[2] for f in range(4))
    reach = max(sum(window(f, faces)[::2]) for f in range(4))
    vmem = pl.BlockSpec(memory_space=pltpu.VMEM)
    anywhere = pl.BlockSpec(memory_space=pl.ANY)
    dma = pltpu.SemaphoreType.DMA
    shapes = (
        jax.ShapeDtypeStruct((3, faces, cases), F32),
        jax.ShapeDtypeStruct((1, cases), F32),
    )
    results = pl.pallas_call(
        functools.partial(kernel, nx, ny),
        out_shape=shapes,
        in_specs=[anywhere] * 3 + [vmem] * 4,
        out_specs=(anywhere, vmem),
        scratch_shapes=[
            pltpu.VMEM((3, faces, cases), F32),
            pltpu.VMEM((interface, interface), BF16),
            pltpu.VMEM((interface, interface), BF16),
            pltpu.VMEM((32, interface), F32),
            pltpu.VMEM((160, reach), BF16),
            pltpu.VMEM((4 * faces, 160), BF16),
            pltpu.VMEM((4, 32, wide), F32),
            pltpu.VMEM((2, faces, cases), F32),
            pltpu.VMEM((2, 1, faces), jnp.int32),
            pltpu.VMEM((EXCHANGES, 4, faces, cases), F32),
            pltpu.VMEM((interface, cases), F32),
            pltpu.VMEM((ITERS, interface, cases), F32),
            pltpu.VMEM((EXCHANGES, interface, cases), F32),
            pltpu.VMEM((SUMS, 1, cases), F32),
            pltpu.VMEM((SUMS, n, 1, cases), F32),
            pltpu.VMEM((8, 128), F32),
            pltpu.VMEM((ny, nx, 8, 128), F32),
            pltpu.VMEM((8, coarse), F32),
            pltpu.VMEM((ny, nx, 8, coarse), F32),
            pltpu.VMEM((slots, slots), BF16),
            pltpu.VMEM((2, slots, slots), BF16),
            pltpu.VMEM((ITERS, 64, cases), F32),
            pltpu.VMEM((ITERS, 64, cases), F32),
            pltpu.VMEM((ITERS, 32, cases), F32),
            pltpu.VMEM((ITERS, nx, 32, cases), F32),
            pltpu.VMEM((ITERS, ny, nx * 8, cases), F32),
            pltpu.VMEM((ITERS, slots, cases), F32),
            pltpu.VMEM((ny, nx, 8, cases), F32),
            pltpu.VMEM((4 * faces, cases), F32),
            pltpu.VMEM((3, faces, cases), F32),
            dma((4,)),
            dma((8,)),
            dma((8,)),
            dma((EXCHANGES, 4)),
            dma((EXCHANGES, 4)),
            dma((SUMS,)),
            dma((SUMS,)),
            dma((4,)),
            dma((4,)),
            dma((ITERS, 3)),
            dma((ITERS, 3)),
            dma((2 * ITERS,)),
            dma((2 * ITERS,)),
        ],
        compiler_params=pltpu.CompilerParams(
            collective_id=0, has_side_effects=True, vmem_limit_bytes=67043328
        ),
    )(
        rhs.reshape(3, faces, cases),
        stiff_inverse.reshape(interface, interface),
        schur.reshape(interface, interface),
        phi.reshape(corners, interface),
        coarse_inverse,
        incidence.reshape(1, nodes),
        pairing.reshape(3, 1, faces),
    )
    multipliers, reduction = pl.pallas_call(
        finish, out_shape=shapes, in_specs=[vmem] * 2, out_specs=(vmem, vmem)
    )(*results)
    return multipliers.reshape(rhs.shape), reduction.reshape(cases)


def solution(mesh):
    nx, ny = mesh.shape["gx"], mesh.shape["gy"]
    return jax.shard_map(
        functools.partial(local, nx, ny),
        mesh=mesh,
        in_specs=(
            P("gx", "gy", None, None, None, None),
            P("gx", "gy", None, None, None),
            P("gx", "gy", None, None, None),
            P("gx", "gy", None, None, None),
            P(("gx", "gy"), None),
            P("gx", "gy", None, None),
            P("gx", "gy", None, None, None),
        ),
        out_specs=(P("gx", "gy", None, None, None, None), P()),
        check_vma=False,
    )
```

time: 65.2 us -> 57 us (0.87)
  local copies, waits for them, and re-layouts: 4.17 us -> 0 us
  Pallas kernels: 60.2 us -> 56.2 us
    unnamed x3 -> x0, local copies, waits for them, and re-layouts: 4.17 us -> none
    pallas_call x1 -> x2, Pallas kernels: 60.2 us -> 56.2 us  [the longest x1 54.5 us: local(): pl.pallas_call(functools.partial(kernel, nx, ny), out_shape=shapes, in_sp...]
where the time goes in v1:
time: 57 us; the launch traced here: 56.8 us
  Pallas kernels  56.2 us (99%)
  between operations  0.64 us (1%)
    pallas_call x1, Pallas kernels, local(): pl.pallas_call(functools.partial(kernel, nx, ny), out_shape=shapes, in_sp...  54.5 us
    pallas_call x1, Pallas kernels, local(): pl.pallas_call(finish, out_shape=shapes, in_specs=[vmem] * 2, out_specs=(...  1.71 us

profile of v1, /device:TPU:0, one launch (start us, length us, event | category | flops | bytes accessed | tf_op | source)
XLA Modules:
  0.0 56.8 jit_solution(6924083685311760067)
XLA Ops:
  0.6 54.5 %shard_map.86 = (f32[3,200,128]{2,1,0:T(8,128)}, f32[1,128]{1,0:T(1,128)}) custom-call(f32[3,200,128]{2,1,0:T(8,128)} %bitcast.10, bf16[1200,1200]{1,0:T(8,128)(2,1)} %bitcast.8, bf16[1200,1200]{1,0:T(8,128)(2,1)} %bitcast.9, bf16[24,1200]{1,0:T(8,128)(2,1)} %bitcast.11, f32[6,192]{1,0:T(8,128)} %cinv_ref.1, s32[1,8]{1,0:T(1,128)} %bitcast.13, ...), custom_call_target="tpu_custom_call" | custom-call | tf_op jit(solution)/shard_map/pallas_call | solution.py:492
  55.1 1.7 %shard_map.87 = (f32[3,200,128]{2,1,0:T(8,128)}, f32[1,128]{1,0:T(1,128)}) custom-call(f32[3,200,128]{2,1,0:T(8,128)} %get-tuple-element.6.mult_ref, f32[1,128]{1,0:T(1,128)} %get-tuple-element.7.reduction_ref), custom_call_target="tpu_custom_call" | custom-call | tf_op jit(solution)/shard_map/pallas_call | solution.py:554

commit v2 on v1

--- a/solution.py
+++ b/solution.py
@@ -10,6 +10,7 @@
 ITERS = 2
 EXCHANGES = 2 * ITERS
 SUMS = 2 * ITERS + 1
+SPLIT = (0, 1, 3)
 MESH = pl.DeviceIdType.MESH
 F32 = jnp.float32
 BF16 = jnp.bfloat16
@@ -48,20 +49,22 @@
 
 
 def kernel(
-    nx, ny, rhs_hbm, stiff_hbm, schur_hbm, phi_ref, cinv_ref, inc_ref, pair_ref,
+    nx, ny, rhs_hbm, stiff_hbm, schur_hbm, phi_hbm, cinv_hbm, inc_hbm, pair_hbm,
     mult_hbm, reduction_ref,
-    rhs_v, stiff, schur, phi_f, spread, spread_t, near_phi, got_rhs, got_pair, got,
-    field, way, image, sums_out, sums_in, ids_out, ids_in, cinv_out, cinv_in, middle, inverse,
+    rhs_v, stiff, schur, phi_ref, cinv_ref, inc_ref, pair_ref, phi_f, spread, spread_t, near_phi, got_rhs, got_pair, got,
+    field, way, image, sums_out, sums_in, cinv_out, cinv_in, middle, inverse,
     part_out, part_in, part_own, load_x, load_y, loads_v, solved, lift, mult_v,
     local_sem, setup_send, setup_recv, face_send, face_recv, sum_send, sum_recv,
     all_send, all_recv, part_send, part_recv, load_send, load_recv,
 ):
     n = nx * ny
     faces = rhs_v.shape[1]
+    interface = stiff.shape[0]
     cases = rhs_v.shape[2]
     jumps = 4 * faces
-    coarse = cinv_in.shape[3]
+    coarse = cinv_hbm.shape[1]
     slots = n * 8
+    span = phi_f.shape[2]
     ix, iy = lax.axis_index("gx"), lax.axis_index("gy")
     me = ix * ny + iy
 
@@ -71,13 +74,12 @@
     across = [at(-1, 0), at(1, 0), at(0, -1), at(0, 1)]
     rows = [pl.ds(f * faces, faces) for f in range(6)]
 
+    sources = [rhs_hbm, pair_hbm, phi_hbm, inc_hbm, cinv_hbm, schur_hbm, stiff_hbm]
+    targets = [rhs_v, pair_ref, phi_ref, inc_ref, cinv_ref, schur, stiff]
     loads = [
-        pltpu.make_async_copy(rhs_hbm, rhs_v, local_sem.at[0]),
-        pltpu.make_async_copy(schur_hbm, schur, local_sem.at[1]),
-        pltpu.make_async_copy(stiff_hbm, stiff, local_sem.at[2]),
+        pltpu.make_async_copy(source, target, local_sem.at[i])
+        for i, (source, target) in enumerate(zip(sources, targets))
     ]
-    for copy in loads:
-        copy.start()
 
     ways_x = [at(d, 0)[0] for d in range(nx)]
     ways_y = [at(0, d)[1] for d in range(ny)]
@@ -99,27 +101,46 @@
 
         lax.fori_loop(1, n, step, 0)
 
+    for copy in loads[:5]:
+        copy.start()
     barrier = pltpu.get_barrier_semaphore()
     each_peer(lambda target: pl.semaphore_signal(
         barrier, inc=1, device_id=target, device_id_type=MESH))
+
+    for copy in loads[5:]:
+        copy.start()
 
     corners = phi_ref.shape[0]
     row = lax.broadcasted_iota(jnp.int32, (32, corners), 0)
     col = lax.broadcasted_iota(jnp.int32, (32, corners), 1)
     point, inner = lax.div(row, 8), lax.rem(row, 8)
     source = 3 * (point + 4 * lax.div(inner, 3)) + lax.rem(inner, 3)
-    order = jnp.where((col == source) & (inner < 6), 1.0, 0.0)
-    phi_f[...] = jnp.dot(order.astype(BF16), phi_ref[...], preferred_element_type=F32)
+    order = jnp.where((col == source) & (inner < 6), 1.0, 0.0).astype(BF16)
+    for i in range(1, 5):
+        loads[i].wait()
+    reach = spread.shape[1]
+    whole_phi = phi_ref[:, pl.ds(0, reach)]
+    spread[pl.ds(0, 32), :] = jnp.dot(
+        order, whole_phi, preferred_element_type=F32
+    ).astype(BF16)
+    for f in range(4):
+        start, offset, width = window(f, faces)
+        piece = phi_ref[:, pl.ds(start, width)].astype(F32)
+        if offset:
+            piece = pltpu.roll(piece, width - offset, axis=1)
+        phi_f[f] = piece[:, 0:span]
     row = lax.broadcasted_iota(jnp.int32, (8, 8), 0)
     col = lax.broadcasted_iota(jnp.int32, (8, 8), 1)
     ids = jnp.broadcast_to(inc_ref[...].astype(F32), (8, 8))
     ids = jnp.sum(jnp.where(col == 4 * lax.div(row, 3), ids, 0.0), axis=1, keepdims=True)
-    row = lax.broadcasted_iota(jnp.int32, ids_out.shape, 0)
-    ids = 3.0 * jnp.broadcast_to(ids, ids_out.shape) + lax.rem(row, 3).astype(F32)
+    wide = cinv_out.shape[1]
+    row = lax.broadcasted_iota(jnp.int32, (8, wide), 0)
+    ids = 3.0 * jnp.broadcast_to(ids, (8, wide)) + lax.rem(row, 3).astype(F32)
     ids = jnp.where(row < 6, ids, -1.0)
-    ids_out[...] = ids
-    ids_in[iy, ix] = ids
     own = jnp.concatenate([cinv_ref[...], jnp.zeros((2, coarse), F32)], axis=0)
+    own = jnp.concatenate([own, jnp.zeros((8, wide - coarse), F32)], axis=1)
+    lanes = lax.broadcasted_iota(jnp.int32, (8, wide), 1)
+    own = jnp.where(lanes == coarse, ids, own)
     cinv_out[...] = own
     cinv_in[iy, ix] = own
 
@@ -153,13 +174,9 @@
         setup.append(send(rhs_v.at[a], got_rhs.at[a], setup_send.at[2 + a],
                           setup_recv.at[2 + a], across[2 * a + 1]))
     for f in range(4):
-        start, _, width = window(f, faces)
-        partner = f ^ 1
-        setup.append(send(phi_f.at[:, pl.ds(start, width)],
-                          near_phi.at[partner, :, pl.ds(0, width)],
-                          setup_send.at[4 + f], setup_recv.at[4 + partner], across[f]))
-    to_line(ids_out, ids_in.at[iy, ix], all_send.at[0], all_recv.at[0], peers_x)
-    to_line(cinv_out, cinv_in.at[iy, ix], all_send.at[1], all_recv.at[1], peers_x)
+        setup.append(send(phi_f.at[f], near_phi.at[f ^ 1], setup_send.at[4 + f],
+                          setup_recv.at[4 + (f ^ 1)], across[f]))
+    to_line(cinv_out, cinv_in.at[iy, ix], all_send.at[0], all_recv.at[0], peers_x)
 
     def turned(pair_row, offset, width):
         lanes = lax.broadcasted_iota(jnp.int32, (1, width), 1)
@@ -193,26 +210,51 @@
                 band, by_col, preferred_element_type=F32
             ).astype(BF16)
 
-    loads[1].wait()
+    loads[5].wait()
     reorder(schur)
 
-    spread[pl.ds(0, 32), :] = phi_f[:, pl.ds(0, spread.shape[1])].astype(BF16)
     for start, width, _, by_col in turns:
         spread[pl.ds(0, 32), pl.ds(start, width)] = jnp.dot(
             spread[pl.ds(0, 32), pl.ds(start, width)], by_col, preferred_element_type=F32
         ).astype(BF16)
     spread[pl.ds(32, 128), :] = jnp.zeros((128, spread.shape[1]), BF16)
 
-    def apply_local(matrix, low, k):
-        sent = []
-        for half in range(3):
-            part = pl.ds(2 * half * faces, 2 * faces)
-            image[k, part, :] = jnp.dot(matrix[part, :], low, preferred_element_type=F32)
-            if half < 2:
-                for f in (2 * half, 2 * half + 1):
-                    sent.append(send(image.at[k, rows[f]], got.at[k, f ^ 1],
-                                     face_send.at[k, f], face_recv.at[k, f ^ 1], across[f]))
-        return sent
+    cut = 2 * faces
+    low_cut, high_cut = cut // 128 * 128, -(-cut // 128) * 128
+
+    def multiply_y(matrix, value, k, part):
+        low = value[cut:].astype(BF16)
+        if cut > low_cut:
+            low = jnp.concatenate([jnp.zeros((cut - low_cut, cases), BF16), low], axis=0)
+        image[k, part, :] = jnp.dot(matrix[part, pl.ds(low_cut, interface - low_cut)], low,
+                                    preferred_element_type=F32)
+
+    def multiply_x(matrix, value, k, part):
+        low = value[0:cut].astype(BF16)
+        if high_cut > cut:
+            low = jnp.concatenate([low, jnp.zeros((high_cut - cut, cases), BF16)], axis=0)
+        image[k, part, :] = image[k, part, :] + jnp.dot(
+            matrix[part, pl.ds(0, high_cut)], low, preferred_element_type=F32)
+
+    def multiply(matrix, value, k, part):
+        image[k, part, :] = jnp.dot(matrix[part, :], value.astype(BF16),
+                                    preferred_element_type=F32)
+
+    last_x = jnp.where(ix == nx - 1, 1, 0)
+
+    def send_faces(k, pair):
+        for f in pair:
+            if f < 2:
+                f = last_x if f == 0 else 1 - last_x
+                part = pl.ds(pl.multiple_of(f * faces, 8), faces)
+                target = lax.rem(ix + 2 * f - 1 + nx, nx)
+                sent.append(send(image.at[k, part], got.at[k, 1 - f], face_send.at[k, f],
+                                 face_recv.at[k, 1 - f], (target, iy)))
+                continue
+            sent.append(send(image.at[k, rows[f]], got.at[k, f ^ 1], face_send.at[k, f],
+                             face_recv.at[k, f ^ 1], across[f]))
+
+    used, masked = pl.ds(0, jumps), pl.ds(jumps, interface - jumps)
 
     def start_sum(partial, k):
         total = jnp.sum(partial, axis=0, keepdims=True)
@@ -224,45 +266,61 @@
         wait_all(sums_in.at[k], sum_recv.at[k])
         return jnp.sum(sums_in[k], axis=0)
 
-    def wait_faces(k):
-        for f in range(4):
+    def wait_faces(k, pair):
+        for f in pair:
             pltpu.make_async_copy(got.at[k, f], got.at[k, f], face_recv.at[k, f]).wait()
 
     zeros = jnp.zeros((2 * faces, cases), F32)
-    for a in range(2):
+    field[pl.ds(jumps, 2 * faces), :] = zeros
+    for k in range(ITERS):
+        way[k, pl.ds(jumps, 2 * faces), :] = zeros
+    sent = []
+
+    def precondition(k, s, ready):
+        ready(1)
+        if k in SPLIT:
+            multiply_y(schur, 0.5 * field[...], k, used)
+        ready(0)
+        half = 0.5 * field[...]
+        if k in SPLIT:
+            multiply_x(schur, half, k, used)
+        else:
+            multiply(schur, half, k, used)
+        start_sum(half[0:jumps] * image[k, used, :], s)
+        if k == EXCHANGES:
+            return
+        send_faces(k, (0, 1))
+        if k == 0:
+            couple()
+        start_loads(k, k // 2)
+        send_faces(k, (2, 3))
+        multiply(schur, half, k, masked)
+
+    def first(a):
         setup[2 + a].wait_recv()
         field[rows[2 * a], :] = -got_rhs[a]
         field[rows[2 * a + 1], :] = rhs_v[a]
-    field[pl.ds(jumps, 2 * faces), :] = zeros
-    for k in range(ITERS):
-        way[k, pl.ds(jumps, 2 * faces), :] = zeros
-
-    sent = []
-
-    def precondition(k, s):
-        half = 0.5 * field[...]
-        sent.extend(apply_local(schur, half.astype(BF16), k))
-        start_sum(half * image[k], s)
 
     def couple():
+        near = []
         for f in range(4):
             setup[4 + (f ^ 1)].wait_recv()
+            other = near_phi[f].astype(BF16)
+            if f % 2:
+                by_col = turned(pair_ref[f // 2], 0, span).astype(BF16)
+                other = jnp.dot(other, by_col, preferred_element_type=F32).astype(BF16)
+            near.append(other)
+        near = jnp.dot(order, jnp.concatenate(near, axis=1), preferred_element_type=F32)
+        for f in range(4):
             start, offset, width = window(f, faces)
-            _, other_offset, other_width = window(f ^ 1, faces)
-            other = near_phi[f, :, pl.ds(0, other_width)]
-            if f % 2:
-                by_col = turned(pair_ref[f // 2], other_offset, other_width)
-                other = jnp.dot(other.astype(BF16), by_col.astype(BF16),
-                                preferred_element_type=F32)
-            if other_width < width:
-                other = jnp.concatenate(
-                    [other, jnp.zeros((32, width - other_width), F32)], axis=1
-                )
-            both = other.shape[1]
-            other = pltpu.roll(other, (offset - other_offset) % both, axis=1)
-            lanes = lax.broadcasted_iota(jnp.int32, (32, both), 1)
+            other = near[:, f * span : (f + 1) * span]
+            if span < width:
+                other = jnp.concatenate([other, jnp.zeros((32, width - span), F32)], axis=1)
+            if offset:
+                other = pltpu.roll(other, offset, axis=1)
+            lanes = lax.broadcasted_iota(jnp.int32, (32, width), 1)
             inside = (lanes >= offset) & (lanes < offset + faces)
-            other = jnp.where(inside, -other, 0.0)[:, 0:width]
+            other = jnp.where(inside, -other, 0.0)
             spread[pl.ds(32 + 32 * f, 32), pl.ds(start, width)] = other.astype(BF16)
 
     def start_loads(k, it):
@@ -328,15 +386,14 @@
         lax.fori_loop(0, blocks, step, 0)
 
     def prepare_coarse():
-        wait_all(ids_in, all_recv.at[2])
-        wait_all(cinv_in, all_recv.at[3])
+        wait_all(cinv_in, all_recv.at[1])
         per_y = nx * 8
         group = block // per_y
 
         def order_columns(part, start):
             first = start if isinstance(start, int) else lax.div(start, per_y)
-            raw = cinv_in[pl.ds(first, group)].reshape(block, coarse)
-            dofs = ids_in[...].reshape(slots, 128)[:, 0:1]
+            raw = cinv_in[pl.ds(first, group)].reshape(block, wide)[:, 0:coarse]
+            dofs = cinv_in[...].reshape(slots, wide)[:, coarse : coarse + 1]
             spot = lax.broadcasted_iota(jnp.int32, (slots, coarse), 1).astype(F32)
             pick = jnp.where(spot == dofs, 1.0, 0.0).astype(BF16)
             middle[pl.ds(start, block), :] = lax.dot_general(
@@ -345,7 +402,7 @@
 
         def order_rows(part, start):
             first = start if isinstance(start, int) else lax.div(start, per_y)
-            dofs = ids_in[pl.ds(first, group)].reshape(block, 128)[:, 0:1]
+            dofs = cinv_in[pl.ds(first, group)].reshape(block, wide)[:, coarse : coarse + 1]
             spot = lax.broadcasted_iota(jnp.int32, (block, slots), 1)
             device = lax.div(spot, 8)
             inner = lax.rem(spot, 8)
@@ -395,35 +452,39 @@
         lift[...] = narrow_dot(spread_t[...], jnp.concatenate(pieces, axis=0), 2)
         return jnp.sum(load * solved[...].reshape(slots, cases), axis=0, keepdims=True)
 
-    precondition(0, 0)
-    couple()
+    precondition(0, 0, first)
     energy = start_energy = None
     ratio = None
     alphas = []
     for it in range(ITERS):
         k = 2 * it
-        start_loads(k, it)
         if it == 0:
-            wait_all(ids_in.at[iy], all_recv.at[0])
-            wait_all(cinv_in.at[iy], all_recv.at[1])
-            to_line(ids_in.at[iy], ids_in.at[iy], all_send.at[2], all_recv.at[2], peers_y)
-            to_line(cinv_in.at[iy], cinv_in.at[iy], all_send.at[3], all_recv.at[3], peers_y)
-            loads[2].wait()
+            wait_all(cinv_in.at[iy], all_recv.at[0])
+            to_line(cinv_in.at[iy], cinv_in.at[iy], all_send.at[1], all_recv.at[1], peers_y)
+            loads[6].wait()
             reorder(stiff)
         pass_loads(it)
         if it:
             following = finish_sum(2 * it)
             ratio = following / energy
             energy = following
-        wait_faces(k)
-        for f in range(4):
-            moved = 0.5 * (image[k, rows[f], :] - got[k, f])
-            if it:
-                moved = moved + ratio * way[it - 1, rows[f], :]
-            way[it, rows[f], :] = moved
+        for a in (1, 0):
+            wait_faces(k, (2 * a, 2 * a + 1))
+            for f in (2 * a, 2 * a + 1):
+                moved = 0.5 * (image[k, rows[f], :] - got[k, f])
+                if it:
+                    moved = moved + ratio * way[it - 1, rows[f], :]
+                way[it, rows[f], :] = moved
+            if a and k + 1 in SPLIT:
+                multiply_y(stiff, way[it], k + 1, used)
         walk = way[it]
-        sent.extend(apply_local(stiff, walk.astype(BF16), k + 1))
-        start_sum(walk * image[k + 1], 2 * it + 1)
+        if k + 1 in SPLIT:
+            multiply_x(stiff, walk, k + 1, used)
+        else:
+            multiply(stiff, walk, k + 1, used)
+        start_sum(walk[0:jumps] * image[k + 1, used, :], 2 * it + 1)
+        send_faces(k + 1, range(4))
+        multiply(stiff, walk, k + 1, masked)
         share_loads(it)
         if it == 0:
             prepare_coarse()
@@ -431,16 +492,14 @@
         coarse_part = solve(it, ratio)
         alpha = energy / (finish_sum(2 * it + 1) + coarse_part)
         alphas.append(alpha)
-        wait_faces(k + 1)
-        for f in range(4):
-            jump = (image[k + 1, rows[f], :] - got[k + 1, f]) + lift[rows[f], :]
-            field[rows[f], :] = field[rows[f], :] - alpha * jump
-        if it + 1 < ITERS:
-            precondition(k + 2, 2 * it + 2)
-        else:
-            half = 0.5 * field[...]
-            product = jnp.dot(schur[...], half.astype(BF16), preferred_element_type=F32)
-            start_sum(half * product, 2 * it + 2)
+
+        def moved_on(a, k=k + 1, alpha=alpha):
+            wait_faces(k, (2 * a, 2 * a + 1))
+            for f in (2 * a, 2 * a + 1):
+                jump = (image[k, rows[f], :] - got[k, f]) + lift[rows[f], :]
+                field[rows[f], :] = field[rows[f], :] - alpha * jump
+
+        precondition(k + 2, 2 * it + 2, moved_on)
 
     for a in range(2):
         total = alphas[0] * way[0, rows[2 * a + 1], :]
@@ -448,15 +507,13 @@
             total = total + alphas[it] * way[it, rows[2 * a + 1], :]
         mult_v[a] = total
     mult_v[2] = jnp.zeros(mult_v.shape[1:], F32)
-    result = pltpu.make_async_copy(mult_v, mult_hbm, local_sem.at[3])
+    result = pltpu.make_async_copy(mult_v, mult_hbm, local_sem.at[7])
     result.start()
 
     for copy in setup + sent:
         copy.wait_send()
-    wait_all(ids_in.at[iy], all_send.at[0])
-    wait_all(cinv_in.at[iy], all_send.at[1])
-    wait_all(ids_in, all_send.at[2])
-    wait_all(cinv_in, all_send.at[3])
+    wait_all(cinv_in.at[iy], all_send.at[0])
+    wait_all(cinv_in, all_send.at[1])
     for it in range(ITERS):
         wait_all(load_x.at[it], load_send.at[it])
         wait_all(load_y.at[it], load_send.at[ITERS + it])
@@ -480,7 +537,8 @@
     coarse = coarse_inverse.shape[1]
     nodes = incidence.shape[3]
     slots = 8 * n
-    wide = max(window(f, faces)[2] for f in range(4))
+    span = -(-faces // 128) * 128
+    wide = (coarse // 128 + 1) * 128
     reach = max(sum(window(f, faces)[::2]) for f in range(4))
     vmem = pl.BlockSpec(memory_space=pltpu.VMEM)
     anywhere = pl.BlockSpec(memory_space=pl.ANY)
@@ -492,28 +550,30 @@
     results = pl.pallas_call(
         functools.partial(kernel, nx, ny),
         out_shape=shapes,
-        in_specs=[anywhere] * 3 + [vmem] * 4,
+        in_specs=[anywhere] * 7,
         out_specs=(anywhere, vmem),
         scratch_shapes=[
             pltpu.VMEM((3, faces, cases), F32),
             pltpu.VMEM((interface, interface), BF16),
             pltpu.VMEM((interface, interface), BF16),
-            pltpu.VMEM((32, interface), F32),
+            pltpu.VMEM((corners, interface), BF16),
+            pltpu.VMEM(coarse_inverse.shape, F32),
+            pltpu.VMEM((1, nodes), jnp.int32),
+            pltpu.VMEM((3, 1, faces), jnp.int32),
+            pltpu.VMEM((4, corners, span), F32),
             pltpu.VMEM((160, reach), BF16),
             pltpu.VMEM((4 * faces, 160), BF16),
-            pltpu.VMEM((4, 32, wide), F32),
+            pltpu.VMEM((4, corners, span), F32),
             pltpu.VMEM((2, faces, cases), F32),
             pltpu.VMEM((2, 1, faces), jnp.int32),
             pltpu.VMEM((EXCHANGES, 4, faces, cases), F32),
             pltpu.VMEM((interface, cases), F32),
             pltpu.VMEM((ITERS, interface, cases), F32),
-            pltpu.VMEM((EXCHANGES, interface, cases), F32),
+            pltpu.VMEM((EXCHANGES + 1, interface, cases), F32),
             pltpu.VMEM((SUMS, 1, cases), F32),
             pltpu.VMEM((SUMS, n, 1, cases), F32),
-            pltpu.VMEM((8, 128), F32),
-            pltpu.VMEM((ny, nx, 8, 128), F32),
-            pltpu.VMEM((8, coarse), F32),
-            pltpu.VMEM((ny, nx, 8, coarse), F32),
+            pltpu.VMEM((8, wide), F32),
+            pltpu.VMEM((ny, nx, 8, wide), F32),
             pltpu.VMEM((slots, slots), BF16),
             pltpu.VMEM((2, slots, slots), BF16),
             pltpu.VMEM((ITERS, 64, cases), F32),
@@ -525,15 +585,15 @@
             pltpu.VMEM((ny, nx, 8, cases), F32),
             pltpu.VMEM((4 * faces, cases), F32),
             pltpu.VMEM((3, faces, cases), F32),
-            dma((4,)),
+            dma((8,)),
             dma((8,)),
             dma((8,)),
             dma((EXCHANGES, 4)),
             dma((EXCHANGES, 4)),
             dma((SUMS,)),
             dma((SUMS,)),
-            dma((4,)),
-            dma((4,)),
+            dma((2,)),
+            dma((2,)),
             dma((ITERS, 3)),
             dma((ITERS, 3)),
             dma((2 * ITERS,)),

time: 57 us -> 50.2 us (0.88)
  Pallas kernels: 56.2 us -> 49.4 us
    pallas_call x1, Pallas kernels: 54.5 us -> 47.7 us  [local(): pl.pallas_call(functools.partial(kernel, nx, ny), out_shape=shapes, in_sp...]
where the time goes in v2:
time: 50.2 us; the launch traced here: 50.1 us
  Pallas kernels  49.4 us (98%)
  between operations  0.64 us (1%)
    pallas_call x1, Pallas kernels, local(): pl.pallas_call(functools.partial(kernel, nx, ny), out_shape=shapes, in_sp...  47.7 us
    pallas_call x1, Pallas kernels, local(): pl.pallas_call(finish, out_shape=shapes, in_specs=[vmem] * 2, out_specs=(...  1.71 us

profile of v2, /device:TPU:0, one launch (start us, length us, event | category | flops | bytes accessed | tf_op | source)
XLA Modules:
  0.0 50.1 jit_solution(10593208460574885077)
XLA Ops:
  0.6 47.7 %shard_map.86 = (f32[3,200,128]{2,1,0:T(8,128)}, f32[1,128]{1,0:T(1,128)}) custom-call(f32[3,200,128]{2,1,0:T(8,128)} %bitcast.10, bf16[1200,1200]{1,0:T(8,128)(2,1)} %bitcast.8, bf16[1200,1200]{1,0:T(8,128)(2,1)} %bitcast.9, bf16[24,1200]{1,0:T(8,128)(2,1)} %bitcast.11, f32[6,192]{1,0:T(8,128)} %cinv_hbm.1, s32[1,8]{1,0:T(1,128)} %bitcast.13, ...), custom_call_target="tpu_custom_call" | custom-call | tf_op jit(solution)/shard_map/pallas_call | solution.py:550
  48.4 1.7 %shard_map.87 = (f32[3,200,128]{2,1,0:T(8,128)}, f32[1,128]{1,0:T(1,128)}) custom-call(f32[3,200,128]{2,1,0:T(8,128)} %get-tuple-element.6.mult_ref, f32[1,128]{1,0:T(1,128)} %get-tuple-element.7.reduction_ref), custom_call_target="tpu_custom_call" | custom-call | tf_op jit(solution)/shard_map/pallas_call | solution.py:614

commit v3 on v2

--- a/solution.py
+++ b/solution.py
@@ -10,7 +10,7 @@
 ITERS = 2
 EXCHANGES = 2 * ITERS
 SUMS = 2 * ITERS + 1
-SPLIT = (0, 1, 3)
+SPLIT = (0, *range(1, EXCHANGES, 2))
 MESH = pl.DeviceIdType.MESH
 F32 = jnp.float32
 BF16 = jnp.bfloat16
@@ -220,6 +220,7 @@
     spread[pl.ds(32, 128), :] = jnp.zeros((128, spread.shape[1]), BF16)
 
     cut = 2 * faces
+    ahead = faces // 32 * 8
     low_cut, high_cut = cut // 128 * 128, -(-cut // 128) * 128
 
     def multiply_y(matrix, value, k, part):
@@ -242,15 +243,15 @@
 
     last_x = jnp.where(ix == nx - 1, 1, 0)
 
+    def send_x(k, start, size):
+        for f in (last_x, 1 - last_x):
+            part = pl.ds(pl.multiple_of(f * faces + start, 8), size)
+            target = lax.rem(ix + 2 * f - 1 + nx, nx)
+            sent.append(send(image.at[k, part], got.at[k, 1 - f, pl.ds(start, size)],
+                             face_send.at[k, f], face_recv.at[k, 1 - f], (target, iy)))
+
     def send_faces(k, pair):
         for f in pair:
-            if f < 2:
-                f = last_x if f == 0 else 1 - last_x
-                part = pl.ds(pl.multiple_of(f * faces, 8), faces)
-                target = lax.rem(ix + 2 * f - 1 + nx, nx)
-                sent.append(send(image.at[k, part], got.at[k, 1 - f], face_send.at[k, f],
-                                 face_recv.at[k, 1 - f], (target, iy)))
-                continue
             sent.append(send(image.at[k, rows[f]], got.at[k, f ^ 1], face_send.at[k, f],
                              face_recv.at[k, f ^ 1], across[f]))
 
@@ -282,18 +283,25 @@
             multiply_y(schur, 0.5 * field[...], k, used)
         ready(0)
         half = 0.5 * field[...]
-        if k in SPLIT:
-            multiply_x(schur, half, k, used)
-        else:
-            multiply(schur, half, k, used)
-        start_sum(half[0:jumps] * image[k, used, :], s)
+        act = multiply_x if k in SPLIT else multiply
+        act(schur, half, k, pl.ds(0, cut))
+        if k == 0:
+            send_x(k, 0, faces)
+        elif k < EXCHANGES:
+            send_x(k, 0, ahead)
+        act(schur, half, k, pl.ds(cut, cut))
+        if k:
+            start_sum(half[0:jumps] * image[k, used, :], s)
         if k == EXCHANGES:
             return
-        send_faces(k, (0, 1))
         if k == 0:
             couple()
+        else:
+            send_x(k, ahead, faces - ahead)
         start_loads(k, k // 2)
         send_faces(k, (2, 3))
+        if k == 0:
+            start_sum(half[0:jumps] * image[k, used, :], s)
         multiply(schur, half, k, masked)
 
     def first(a):
@@ -478,12 +486,13 @@
             if a and k + 1 in SPLIT:
                 multiply_y(stiff, way[it], k + 1, used)
         walk = way[it]
-        if k + 1 in SPLIT:
-            multiply_x(stiff, walk, k + 1, used)
-        else:
-            multiply(stiff, walk, k + 1, used)
+        act = multiply_x if k + 1 in SPLIT else multiply
+        act(stiff, walk, k + 1, pl.ds(0, cut))
+        send_x(k + 1, 0, ahead)
+        act(stiff, walk, k + 1, pl.ds(cut, cut))
         start_sum(walk[0:jumps] * image[k + 1, used, :], 2 * it + 1)
-        send_faces(k + 1, range(4))
+        send_x(k + 1, ahead, faces - ahead)
+        send_faces(k + 1, (2, 3))
         multiply(stiff, walk, k + 1, masked)
         share_loads(it)
         if it == 0:

time: 50.2 us -> 49.4 us (0.984)
  Pallas kernels: 49.4 us -> 48.6 us
    pallas_call x1, Pallas kernels: 47.7 us -> 46.9 us  [local(): pl.pallas_call(functools.partial(kernel, nx, ny), out_shape=shapes, in_sp...]
where the time goes in v3:
time: 49.4 us; the launch traced here: 49.2 us
  Pallas kernels  48.6 us (98%)
  between operations  0.64 us (1%)
    pallas_call x1, Pallas kernels, local(): pl.pallas_call(functools.partial(kernel, nx, ny), out_shape=shapes, in_sp...  46.9 us
    pallas_call x1, Pallas kernels, local(): pl.pallas_call(finish, out_shape=shapes, in_specs=[vmem] * 2, out_specs=(...  1.71 us

profile of v3, /device:TPU:0, one launch (start us, length us, event | category | flops | bytes accessed | tf_op | source)
XLA Modules:
  0.0 49.2 jit_solution(13765479284703120540)
XLA Ops:
  0.6 46.9 %shard_map.86 = (f32[3,200,128]{2,1,0:T(8,128)}, f32[1,128]{1,0:T(1,128)}) custom-call(f32[3,200,128]{2,1,0:T(8,128)} %bitcast.10, bf16[1200,1200]{1,0:T(8,128)(2,1)} %bitcast.8, bf16[1200,1200]{1,0:T(8,128)(2,1)} %bitcast.9, bf16[24,1200]{1,0:T(8,128)(2,1)} %bitcast.11, f32[6,192]{1,0:T(8,128)} %cinv_hbm.1, s32[1,8]{1,0:T(1,128)} %bitcast.13, ...), custom_call_target="tpu_custom_call" | custom-call | tf_op jit(solution)/shard_map/pallas_call | solution.py:559
  47.5 1.7 %shard_map.87 = (f32[3,200,128]{2,1,0:T(8,128)}, f32[1,128]{1,0:T(1,128)}) custom-call(f32[3,200,128]{2,1,0:T(8,128)} %get-tuple-element.6.mult_ref, f32[1,128]{1,0:T(1,128)} %get-tuple-element.7.reduction_ref), custom_call_target="tpu_custom_call" | custom-call | tf_op jit(solution)/shard_map/pallas_call | solution.py:623

commit v4 on v3

--- a/solution.py
+++ b/solution.py
@@ -365,17 +365,20 @@
         line = part_own[it] + part_in[it, pl.ds(0, 32), :]
         inner = part_in[it, pl.ds(32, 16), :] + part_in[it, pl.ds(48, 16), :]
         edge = jnp.zeros((8, cases), F32)
-        load_x[it, ix] = line + jnp.concatenate([edge, inner, edge], axis=0)
+        total = line + jnp.concatenate([edge, inner, edge], axis=0)
+        load_x[it, ix] = jnp.concatenate([total[8 * a : 8 * a + 6] for a in range(4)], axis=0)
         to_line(load_x.at[it, ix], load_x.at[it, ix], load_send.at[it], load_recv.at[it],
                 peers_x)
 
     def share_loads(it):
         wait_all(load_x.at[it], load_recv.at[it])
+        lines = [load_x[it, x] for x in range(nx)]
         for x in range(nx):
-            total = load_x[it, (x + 1) % nx, pl.ds(0, 8), :]
+            total = lines[(x + 1) % nx][0:6]
             for a in range(3):
-                total = total + load_x[it, (x - a) % nx, pl.ds(8 * a + 8, 8), :]
-            load_y[it, iy, pl.ds(8 * x, 8), :] = total
+                total = total + lines[(x - a) % nx][6 * a + 6 : 6 * a + 12]
+            load_y[it, iy, pl.ds(8 * x, 8), :] = jnp.concatenate(
+                [total, jnp.zeros((2, cases), F32)], axis=0)
         to_line(load_y.at[it, iy], load_y.at[it, iy], load_send.at[ITERS + it],
                 load_recv.at[ITERS + it], peers_y)
 
@@ -588,7 +591,7 @@
             pltpu.VMEM((ITERS, 64, cases), F32),
             pltpu.VMEM((ITERS, 64, cases), F32),
             pltpu.VMEM((ITERS, 32, cases), F32),
-            pltpu.VMEM((ITERS, nx, 32, cases), F32),
+            pltpu.VMEM((ITERS, nx, 24, cases), F32),
             pltpu.VMEM((ITERS, ny, nx * 8, cases), F32),
             pltpu.VMEM((ITERS, slots, cases), F32),
             pltpu.VMEM((ny, nx, 8, cases), F32),

time: 49.4 us -> 49.4 us (level)
  no operation moved by 1% of the time
where the time goes in v4:
time: 49.4 us; the launch traced here: 49.2 us
  Pallas kernels  48.6 us (98%)
  between operations  0.64 us (1%)
    pallas_call x1, Pallas kernels, local(): pl.pallas_call(functools.partial(kernel, nx, ny), out_shape=shapes, in_sp...  46.9 us
    pallas_call x1, Pallas kernels, local(): pl.pallas_call(finish, out_shape=shapes, in_specs=[vmem] * 2, out_specs=(...  1.71 us

profile of v4, /device:TPU:0, one launch (start us, length us, event | category | flops | bytes accessed | tf_op | source)
XLA Modules:
  0.0 49.2 jit_solution(13768577814674465951)
XLA Ops:
  0.6 46.9 %shard_map.86 = (f32[3,200,128]{2,1,0:T(8,128)}, f32[1,128]{1,0:T(1,128)}) custom-call(f32[3,200,128]{2,1,0:T(8,128)} %bitcast.10, bf16[1200,1200]{1,0:T(8,128)(2,1)} %bitcast.8, bf16[1200,1200]{1,0:T(8,128)(2,1)} %bitcast.9, bf16[24,1200]{1,0:T(8,128)(2,1)} %bitcast.11, f32[6,192]{1,0:T(8,128)} %cinv_hbm.1, s32[1,8]{1,0:T(1,128)} %bitcast.13, ...), custom_call_target="tpu_custom_call" | custom-call | tf_op jit(solution)/shard_map/pallas_call | solution.py:562
  47.5 1.7 %shard_map.87 = (f32[3,200,128]{2,1,0:T(8,128)}, f32[1,128]{1,0:T(1,128)}) custom-call(f32[3,200,128]{2,1,0:T(8,128)} %get-tuple-element.6.mult_ref, f32[1,128]{1,0:T(1,128)} %get-tuple-element.7.reduction_ref), custom_call_target="tpu_custom_call" | custom-call | tf_op jit(solution)/shard_map/pallas_call | solution.py:626
